TPU v7x, 32 devices: a whole 2x2x4 slice. The times are simulated.
32 devices in a mesh: dp: 8 (over z, y), head: 4 (over x, core).
Axes of the slice: x: 2, y: 2, z: 4, core: 2. Of those that a mesh axis runs over, the one named last changes fastest.
Arguments:
- tokens: bfloat16 [8, 6312, 768], P('dp', 'head'), may hold values from -6 to 6
- frames: int32 [8], P('dp'), may hold values from 4 to 16
- text_mask: int32 [8, 40], P('dp'), may hold values 0 or 1
- latents: bfloat16 [8, 128, 768], P('dp'), may hold values from -6 to 6
- cross_q: bfloat16 [768, 768], P('head'), may hold values from -0.21875 to 0.21875
- cross_kv: bfloat16 [2, 768, 768], P(None, 'head'), may hold values from -0.21875 to 0.21875
- cross_out: bfloat16 [768, 768], P('head'), may hold values from -3.5 to 3.5
- cross_up: bfloat16 [768, 3072], P(None, 'head'), may hold values from -0.21875 to 0.21875
- cross_down: bfloat16 [3072, 768], P('head'), may hold values from -0.109375 to 0.109375
- self_qkv: bfloat16 [3, 768, 768], P(None, 'head'), may hold values from -0.21875 to 0.21875
- self_out: bfloat16 [768, 768], P('head'), may hold values from -0.875 to 0.875
- self_up: bfloat16 [768, 3072], P(None, 'head'), may hold values from -0.21875 to 0.21875
- self_down: bfloat16 [3072, 768], P('head'), may hold values from -0.109375 to 0.109375
- head_bias: float32 [2, 2, 768], P(None, None, 'head'), may hold values from -1.8 to 1.8
- up_bias: float32 [2, 3072], P(None, 'head'), may hold values from -1.8 to 1.8
- out_bias: float32 [2, 2, 768], replicated, may hold values from -1.8 to 1.8
- norm_gain: float32 [5, 768], replicated, may hold values from 0.5 to 1.5
- norm_bias: float32 [5, 768], replicated, may hold values from -1.8 to 1.8
- latents_cot: float32 [8, 128, 768], P('dp'), may hold values from -6 to 6
Outputs:
- latents_out: float32 [8, 128, 768], P('dp')
- grad_tokens: bfloat16 [8, 6312, 768], P('dp', 'head')
- grad_latents: float32 [8, 128, 768], P('dp')
- grad_cross_q: float32 [768, 768], P('head', 'dp')
- grad_cross_kv: float32 [2, 768, 768], P(None, 'head', 'dp')
- grad_cross_out: float32 [768, 768], P('head', 'dp')
- grad_cross_up: float32 [768, 3072], P('dp', 'head')
- grad_cross_down: float32 [3072, 768], P('head', 'dp')
- grad_self_qkv: float32 [3, 768, 768], P(None, 'head', 'dp')
- grad_self_out: float32 [768, 768], P('head', 'dp')
- grad_self_up: float32 [768, 3072], P('dp', 'head')
- grad_self_down: float32 [3072, 768], P('head', 'dp')
- grad_head_bias: float32 [2, 2, 768], P(None, None, 'head')
- grad_up_bias: float32 [2, 3072], P(None, 'head')
- grad_out_bias: float32 [2, 2, 768], P(None, None, 'head')
- grad_norm_gain: float32 [5, 768], P(None, 'head')
- grad_norm_bias: float32 [5, 768], P(None, 'head')
Inputs may be any that keep to these rules, and one draw needn't show every extreme that they name: The patches of frames at or after frames[c] are padding.
All inputs are finite; a program needn't handle non-finite values. No bound on the sum of `text_mask` on one device may be relied on, other than what follows from the above.
Results may differ from a plain program's by a relative error of at most 0.018.
Values may be sent and summed in bfloat16 or wider, within the bound.
A program may use at most 128 MiB of HBM per device.

v0:
```python
from functools import partial

import jax
import jax.numpy as jnp
from jax import lax
from jax.sharding import PartitionSpec as P

HD = 64
P_SIZE = 392
F_MAX = 16


EPSILON = 1e-05
NEGATIVE = -1e30


def normed(tensor, gain_row, shift_row):
    row_mean = jnp.mean(tensor, axis=-1, keepdims=True)
    centered = tensor - row_mean
    spread = jnp.mean(centered * centered, axis=-1, keepdims=True)
    return centered * lax.rsqrt(spread + EPSILON) * gain_row + shift_row


def share_of(tensor, head_index, head_width):
    return lax.dynamic_slice_in_dim(tensor, head_index * head_width, head_width, tensor.ndim - 1)


def split_heads(tensor, heads_here):
    return tensor.reshape(
        tensor.shape[0], tensor.shape[1], heads_here, tensor.shape[2] // heads_here
    )


def merge_heads(tensor):
    return tensor.reshape(tensor.shape[0], tensor.shape[1], tensor.shape[2] * tensor.shape[3])


def join_heads(partial_sum):
    return lax.psum(partial_sum.astype(jnp.bfloat16), "head").astype(jnp.float32)


def join_back(partial_sum):
    return lax.psum(partial_sum.astype(jnp.bfloat16), "head").astype(jnp.float32)


def scores_of(queries, key_rows, usable):
    scores = jnp.einsum("qhe,khe->hqk", queries, key_rows, preferred_element_type=jnp.float32)
    return jnp.where(usable[None, None, :], scores, NEGATIVE)


def attend_parts(parts):
    queries, key_rows, values, usable = parts
    scores = scores_of(queries, key_rows, usable)
    row_max = jnp.max(scores, axis=-1, keepdims=True)
    powers = jnp.exp(scores - row_max)
    totals = jnp.sum(powers, axis=-1, keepdims=True)
    chances = (powers / totals).astype(jnp.bfloat16)
    mixture = jnp.einsum("hqk,khe->qhe", chances, values, preferred_element_type=jnp.float32)
    return (mixture.astype(jnp.bfloat16), row_max, totals)


def back_parts(parts):
    queries, key_rows, values, usable, row_max, totals, grad_mix = parts
    scores = scores_of(queries, key_rows, usable)
    chances = jnp.exp(scores - row_max) / totals
    rounded = chances.astype(jnp.bfloat16)
    grad_values = jnp.einsum(
        "hqk,qhe->khe", rounded, grad_mix, preferred_element_type=jnp.float32
    ).astype(jnp.bfloat16)
    grad_chances = jnp.einsum("qhe,khe->hqk", grad_mix, values, preferred_element_type=jnp.float32)
    inner_sum = jnp.sum(chances * grad_chances, axis=-1, keepdims=True)
    grad_scores = (chances * (grad_chances - inner_sum)).astype(jnp.bfloat16)
    grad_queries = jnp.einsum(
        "hqk,khe->qhe", grad_scores, key_rows, preferred_element_type=jnp.float32
    ).astype(jnp.bfloat16)
    grad_keys = jnp.einsum(
        "hqk,qhe->khe", grad_scores, queries, preferred_element_type=jnp.float32
    ).astype(jnp.bfloat16)
    return (grad_queries, grad_keys, grad_values)


def feed_forward(tensor, gain_row, shift_row, weight_up, bias_up, weight_down):
    hidden = normed(tensor, gain_row, shift_row).astype(jnp.bfloat16)
    pre_act = (
        jnp.einsum("cnd,df->cnf", hidden, weight_up, preferred_element_type=jnp.float32) + bias_up
    )
    activation = jax.nn.gelu(pre_act, approximate=True).astype(jnp.bfloat16)
    partial_sum = jnp.einsum(
        "cnf,fd->cnd", activation, weight_down, preferred_element_type=jnp.float32
    )
    return (join_heads(partial_sum), (hidden, pre_act, activation))


def feed_back(tensor, gain_row, shift_row, weight_up, weight_down, saved_acts, grad_out):
    hidden, pre_act, activation = saved_acts
    grad_branch = grad_out.astype(jnp.bfloat16)
    grad_weight_down = jnp.einsum(
        "cnf,cnd->fd", activation, grad_branch, preferred_element_type=jnp.float32
    )
    grad_act = jnp.einsum(
        "cnd,fd->cnf", grad_branch, weight_down, preferred_element_type=jnp.float32
    )
    unused, gelu_pull = jax.vjp(partial(jax.nn.gelu, approximate=True), pre_act)
    grad_pre = gelu_pull(grad_act)[0].astype(jnp.bfloat16)
    grad_weight_up = jnp.einsum("cnd,cnf->df", hidden, grad_pre, preferred_element_type=jnp.float32)
    grad_bias_up = jnp.sum(grad_pre.astype(jnp.float32), axis=(0, 1))
    grad_hidden = join_back(
        jnp.einsum("cnf,df->cnd", grad_pre, weight_up, preferred_element_type=jnp.float32)
    )
    unused_too, norm_pull = jax.vjp(normed, tensor, gain_row, shift_row)
    grad_tensor, grad_gain, grad_shift = norm_pull(grad_hidden)
    return (grad_tensor, grad_weight_up, grad_bias_up, grad_weight_down, grad_gain, grad_shift)


def local(
    tokens,
    frames,
    text_mask,
    latents,
    cross_q,
    cross_kv,
    cross_out,
    cross_up,
    cross_down,
    self_qkv,
    self_out,
    self_up,
    self_down,
    head_bias,
    up_bias,
    out_bias,
    norm_gain,
    norm_bias,
    latents_cot,
):
    head_index = lax.axis_index("head")
    head_width = cross_q.shape[0]
    heads_here = head_width // HD
    scaling = HD ** (-0.5)
    clips_here = tokens.shape[0]
    rows_here = tokens.shape[1]
    length = rows_here * lax.axis_size("head")
    position = jnp.arange(length, dtype=jnp.int32)
    text_full = jnp.concatenate(
        [jnp.zeros((clips_here, F_MAX * P_SIZE), jnp.int32), text_mask], axis=1
    )
    usable = (position[None, :] < frames[:, None] * P_SIZE) | (text_full == 1)
    gathered, weights_whole = (
        lax.all_gather(tokens, "head", axis=1, tiled=True),
        lax.all_gather(cross_kv, "head", axis=1, tiled=True),
    )
    full_rows = gathered.astype(jnp.float32)
    row_mean = jnp.mean(full_rows, axis=-1, keepdims=True)
    centered = full_rows - row_mean
    inverse = lax.rsqrt(jnp.mean(centered * centered, axis=-1, keepdims=True) + EPSILON)
    inputs = (centered * inverse * norm_gain[0] + norm_bias[0]).astype(jnp.bfloat16)
    key_value = jnp.einsum("cld,kwd->clkw", inputs, cross_kv, preferred_element_type=jnp.float32)
    key_rows = key_value[:, :, 0].astype(jnp.bfloat16)
    cross_values = (key_value[:, :, 1] + head_bias[0, 1]).astype(jnp.bfloat16)
    start_state = latents.astype(jnp.float32)
    latent_norm = normed(start_state, norm_gain[1], norm_bias[1]).astype(jnp.bfloat16)
    cross_queries = (
        (
            jnp.einsum("cnd,wd->cnw", latent_norm, cross_q, preferred_element_type=jnp.float32)
            + head_bias[0, 0]
        )
        * scaling
    ).astype(jnp.bfloat16)
    cross_parts = (
        split_heads(cross_queries, heads_here),
        split_heads(key_rows, heads_here),
        split_heads(cross_values, heads_here),
        usable,
    )
    cross_mix, cross_max, cross_totals = lax.map(attend_parts, cross_parts)
    cross_flat = merge_heads(cross_mix)
    after_cross = (
        start_state
        + join_heads(
            jnp.einsum("cnw,wd->cnd", cross_flat, cross_out, preferred_element_type=jnp.float32)
        )
        + out_bias[0, 0]
    )
    cross_branch, cross_saved = feed_forward(
        after_cross, norm_gain[2], norm_bias[2], cross_up, up_bias[0], cross_down
    )
    after_mlp = after_cross + cross_branch + out_bias[0, 1]
    self_norm = normed(after_mlp, norm_gain[3], norm_bias[3]).astype(jnp.bfloat16)
    triple = jnp.einsum("cnd,kwd->cnkw", self_norm, self_qkv, preferred_element_type=jnp.float32)
    self_queries = ((triple[:, :, 0] + head_bias[1, 0]) * scaling).astype(jnp.bfloat16)
    self_keys = triple[:, :, 1].astype(jnp.bfloat16)
    self_values = (triple[:, :, 2] + head_bias[1, 1]).astype(jnp.bfloat16)
    everyone = jnp.ones((clips_here, self_keys.shape[1]), dtype=bool)
    self_parts = (
        split_heads(self_queries, heads_here),
        split_heads(self_keys, heads_here),
        split_heads(self_values, heads_here),
        everyone,
    )
    self_mix, self_max, self_totals = lax.map(attend_parts, self_parts)
    self_flat = merge_heads(self_mix)
    after_self = (
        after_mlp
        + join_heads(
            jnp.einsum("cnw,wd->cnd", self_flat, self_out, preferred_element_type=jnp.float32)
        )
        + out_bias[1, 0]
    )
    self_branch, self_saved = feed_forward(
        after_self, norm_gain[4], norm_bias[4], self_up, up_bias[1], self_down
    )
    latents_out = after_self + self_branch + out_bias[1, 1]
    bias_self_mlp = jnp.sum(latents_cot, axis=(0, 1))
    grad_ln_four, grad_self_up, upbias_self, grad_self_down, gain_four, shift_four = feed_back(
        after_self, norm_gain[4], norm_bias[4], self_up, self_down, self_saved, latents_cot
    )
    grad_state = latents_cot + grad_ln_four
    bias_self_attn = jnp.sum(grad_state, axis=(0, 1))
    grad_attn_in = grad_state.astype(jnp.bfloat16)
    grad_self_out = jnp.einsum(
        "cnw,cnd->wd", self_flat, grad_attn_in, preferred_element_type=jnp.float32
    )
    grad_mix = jnp.einsum(
        "cnd,wd->cnw", grad_attn_in, self_out, preferred_element_type=jnp.float32
    ).astype(jnp.bfloat16)
    self_grads = lax.map(
        back_parts, self_parts + (self_max, self_totals, split_heads(grad_mix, heads_here))
    )
    grad_query_scaled = (merge_heads(self_grads[0]).astype(jnp.float32) * scaling).astype(
        jnp.bfloat16
    )
    grad_triple = jnp.stack(
        [grad_query_scaled, merge_heads(self_grads[1]), merge_heads(self_grads[2])], axis=2
    )
    grad_self_qkv = jnp.einsum(
        "cnd,cnkw->kwd", self_norm, grad_triple, preferred_element_type=jnp.float32
    )
    bias_self_q = jnp.sum(grad_triple[:, :, 0].astype(jnp.float32), axis=(0, 1))
    bias_self_v = jnp.sum(grad_triple[:, :, 2].astype(jnp.float32), axis=(0, 1))
    grad_self_in = join_back(
        jnp.einsum("cnkw,kwd->cnd", grad_triple, self_qkv, preferred_element_type=jnp.float32)
    )
    unused, norm_pull = jax.vjp(normed, after_mlp, norm_gain[3], norm_bias[3])
    grad_ln_three, gain_three, shift_three = norm_pull(grad_self_in)
    grad_state = grad_state + grad_ln_three
    bias_cross_mlp = jnp.sum(grad_state, axis=(0, 1))
    grad_ln_two, grad_cross_up, upbias_cross, grad_cross_down, gain_two, shift_two = feed_back(
        after_cross, norm_gain[2], norm_bias[2], cross_up, cross_down, cross_saved, grad_state
    )
    grad_state = grad_state + grad_ln_two
    bias_cross_attn = jnp.sum(grad_state, axis=(0, 1))
    grad_attn_in = grad_state.astype(jnp.bfloat16)
    grad_cross_out = jnp.einsum(
        "cnw,cnd->wd", cross_flat, grad_attn_in, preferred_element_type=jnp.float32
    )
    grad_mix = jnp.einsum(
        "cnd,wd->cnw", grad_attn_in, cross_out, preferred_element_type=jnp.float32
    ).astype(jnp.bfloat16)
    cross_grads = lax.map(
        back_parts, cross_parts + (cross_max, cross_totals, split_heads(grad_mix, heads_here))
    )
    grad_query_cross = (merge_heads(cross_grads[0]).astype(jnp.float32) * scaling).astype(
        jnp.bfloat16
    )
    grad_cross_q = jnp.einsum(
        "cnd,cnw->wd", latent_norm, grad_query_cross, preferred_element_type=jnp.float32
    )
    bias_cross_q = jnp.sum(grad_query_cross.astype(jnp.float32), axis=(0, 1))
    grad_latent_in = join_back(
        jnp.einsum("cnw,wd->cnd", grad_query_cross, cross_q, preferred_element_type=jnp.float32)
    )
    unused_too, latent_pull = jax.vjp(normed, start_state, norm_gain[1], norm_bias[1])
    grad_ln_one, gain_one, shift_one = latent_pull(grad_latent_in)
    grad_latents = grad_state + grad_ln_one
    grad_pair = jnp.stack([merge_heads(cross_grads[1]), merge_heads(cross_grads[2])], axis=2)
    grad_cross_kv = jnp.einsum(
        "cld,clkw->kwd", inputs, grad_pair, preferred_element_type=jnp.float32
    )
    bias_cross_v = jnp.sum(grad_pair[:, :, 1].astype(jnp.float32), axis=(0, 1))
    arrived = lax.all_to_all(grad_pair, "head", split_axis=1, concat_axis=3, tiled=True)
    grad_share = jnp.einsum(
        "clkw,kwd->cld", arrived, weights_whole, preferred_element_type=jnp.float32
    )
    own_start = head_index * rows_here
    own_mean = lax.dynamic_slice_in_dim(row_mean, own_start, rows_here, 1)
    own_inverse = lax.dynamic_slice_in_dim(inverse, own_start, rows_here, 1)
    standard = (tokens.astype(jnp.float32) - own_mean) * own_inverse
    scaled = grad_share * norm_gain[0]
    mean_plain = jnp.mean(scaled, axis=-1, keepdims=True)
    mean_cross = jnp.mean(scaled * standard, axis=-1, keepdims=True)
    grad_tokens = (own_inverse * (scaled - mean_plain - standard * mean_cross)).astype(jnp.bfloat16)
    gain_zero, shift_zero = lax.psum(
        (jnp.sum(grad_share * standard, axis=(0, 1)), jnp.sum(grad_share, axis=(0, 1))), "head"
    )
    grad_head_bias = jnp.stack(
        [jnp.stack([bias_cross_q, bias_cross_v]), jnp.stack([bias_self_q, bias_self_v])]
    )
    grad_up_bias = jnp.stack([upbias_cross, upbias_self])
    out_full = jnp.stack(
        [jnp.stack([bias_cross_attn, bias_cross_mlp]), jnp.stack([bias_self_attn, bias_self_mlp])]
    )
    grad_out_bias = share_of(out_full, head_index, head_width)
    grad_norm_gain = share_of(
        jnp.stack([gain_zero, gain_one, gain_two, gain_three, gain_four]), head_index, head_width
    )
    grad_norm_bias = share_of(
        jnp.stack([shift_zero, shift_one, shift_two, shift_three, shift_four]),
        head_index,
        head_width,
    )
    small_sums = lax.psum(
        (grad_head_bias, grad_up_bias, grad_out_bias, grad_norm_gain, grad_norm_bias), "dp"
    )
    combined = (
        lax.psum_scatter(grad_cross_q, "dp", scatter_dimension=1, tiled=True),
        lax.psum_scatter(grad_cross_kv, "dp", scatter_dimension=2, tiled=True),
        lax.psum_scatter(grad_cross_out, "dp", scatter_dimension=1, tiled=True),
        lax.psum_scatter(grad_cross_up, "dp", scatter_dimension=0, tiled=True),
        lax.psum_scatter(grad_cross_down, "dp", scatter_dimension=1, tiled=True),
        lax.psum_scatter(grad_self_qkv, "dp", scatter_dimension=2, tiled=True),
        lax.psum_scatter(grad_self_out, "dp", scatter_dimension=1, tiled=True),
        lax.psum_scatter(grad_self_up, "dp", scatter_dimension=0, tiled=True),
        lax.psum_scatter(grad_self_down, "dp", scatter_dimension=1, tiled=True),
    )
    cross_sums = combined[:5]
    self_sums = combined[5:]
    return (
        latents_out,
        grad_tokens,
        grad_latents,
        cross_sums[0],
        cross_sums[1],
        cross_sums[2],
        cross_sums[3],
        cross_sums[4],
        self_sums[0],
        self_sums[1],
        self_sums[2],
        self_sums[3],
        small_sums[0],
        small_sums[1],
        small_sums[2],
        small_sums[3],
        small_sums[4],
    )


def solution(mesh):
    in_specs = (
        P("dp", "head", None),
        P("dp"),
        P("dp", None),
        P("dp", None, None),
        P("head", None),
        P(None, "head", None),
        P("head", None),
        P(None, "head"),
        P("head", None),
        P(None, "head", None),
        P("head", None),
        P(None, "head"),
        P("head", None),
        P(None, None, "head"),
        P(None, "head"),
        P(),
        P(),
        P(),
        P("dp", None, None),
    )
    out_specs = (
        P("dp", None, None),
        P("dp", "head", None),
        P("dp", None, None),
        P("head", "dp"),
        P(None, "head", "dp"),
        P("head", "dp"),
        P("dp", "head"),
        P("head", "dp"),
        P(None, "head", "dp"),
        P("head", "dp"),
        P("dp", "head"),
        P("head", "dp"),
        P(None, None, "head"),
        P(None, "head"),
        P(None, None, "head"),
        P(None, "head"),
        P(None, "head"),
    )
    return jax.shard_map(local, mesh=mesh, in_specs=in_specs, out_specs=out_specs, check_vma=False)
```

profile of v0, /device:TPU:0, one launch (start us, length us, event | category | flops | bytes accessed | tf_op | source)
XLA Modules:
  0.0 1166.3 jit_solution(2360226538765348507)
XLA Ops:
  7.3 18.4 %copy.55 = bf16[1,1578,768]{2,0,1:T(2,128)(2,1)} copy(bf16[1,1578,768]{2,1,0:T(8,128)(2,1)} %param.19) | data formatting | bytes 4847616 | tf_op args[0]
  28.8 122.7 %all-gather.3.cloned.1.call-done = bf16[1,6312,768]{2,0,1:T(2,128)(2,1)} async-done(((bf16[1,1578,768]{2,0,1:T(2,128)(2,1)}), bf16[1,6312,768]{2,0,1:T(2,128)(2,1)}) %all-gather.3.cloned.1.call-update) | async-done | bytes 9695248 | tf_op jit(solution)/shard_map/all_gather | solution.py:149
  159.0 14.1 %fusion.4 = f32[6312]{0:T(1024)S(1)} fusion(f32[6312]{0:T(1024)S(1)} %broadcast_multiply_fusion, bf16[1,6312,768]{2,0,1:T(2,128)(2,1)} %all-gather.3.cloned.1.call-done), kind=kLoop, calls=%fused_computation.6 | loop fusion | flops 19384152 | bytes 9745728 | tf_op jit(solution)/shard_map/reduce_sum | solution.py:155
  201.4 31.3 %all-reduce.12.cloned.1.call-done = bf16[1,128,768]{2,1,0:T(8,128)(2,1)} async-done(((bf16[1,128,768]{2,1,0:T(8,128)(2,1)}), bf16[1,128,768]{2,1,0:T(8,128)(2,1)}) %all-reduce.12.cloned.1.call-update) | async-done | bytes 196624 | tf_op jit(solution)/shard_map/psum | solution.py:39
  239.6 30.8 %all-reduce.14.cloned.1.call-done = bf16[1,128,768]{2,1,0:T(8,128)(2,1)} async-done(((bf16[1,128,768]{2,1,0:T(8,128)(2,1)}), bf16[1,128,768]{2,1,0:T(8,128)(2,1)}) %all-reduce.14.cloned.1.call-update) | async-done | bytes 196624 | tf_op jit(solution)/shard_map/psum | solution.py:39
  280.2 32.1 %all-reduce.16.cloned.1.call-done = bf16[1,128,768]{2,1,0:T(8,128)(2,1)} async-done(((bf16[1,128,768]{2,1,0:T(8,128)(2,1)}), bf16[1,128,768]{2,1,0:T(8,128)(2,1)}) %all-reduce.16.cloned.1.call-update) | async-done | bytes 196624 | tf_op jit(solution)/shard_map/psum | solution.py:39
  320.6 32.1 %all-reduce.18.cloned.1.call-done = bf16[1,128,768]{2,1,0:T(8,128)(2,1)} async-done(((bf16[1,128,768]{2,1,0:T(8,128)(2,1)}), bf16[1,128,768]{2,1,0:T(8,128)(2,1)}) %all-reduce.18.cloned.1.call-update) | async-done | bytes 196624 | tf_op jit(solution)/shard_map/psum | solution.py:43
  369.2 32.1 %all-reduce.20.cloned.1.call-done = bf16[1,128,768]{2,1,0:T(8,128)(2,1)} async-done(((bf16[1,128,768]{2,1,0:T(8,128)(2,1)}), bf16[1,128,768]{2,1,0:T(8,128)(2,1)}) %all-reduce.20.cloned.1.call-update) | async-done | bytes 196624 | tf_op jit(solution)/shard_map/psum | solution.py:43
  412.8 29.3 %all-reduce.22.cloned.1.call-done = bf16[1,128,768]{2,1,0:T(8,128)(2,1)} async-done(((bf16[1,128,768]{2,1,0:T(8,128)(2,1)}), bf16[1,128,768]{2,1,0:T(8,128)(2,1)}) %all-reduce.22.cloned.1.call-update) | async-done | bytes 196624 | tf_op jit(solution)/shard_map/psum | solution.py:43
  447.5 11.8 %multiply_reduce_fusion = (f32[3,128]{1,0:T(4,128)S(1)}, f32[3,128,6312]{1,2,0:T(8,128)}) fusion(f32[3,128,6312]{1,2,0:T(8,128)} %get-tuple-element.188, f32[3,128]{1,0:T(4,128)S(1)} %copy-done.84, bf16[128,3,64]{0,2,1:T(8,128)(2,1)S(1)} %bitcast.256, f32[6312,3,64]{0,2,1:T(8,128)} %bitcast.227, f32[3,64]{1,0:T(4,128)S(1)} %copy-done.93), kind=kOutput, calls=%fused_computation.16 | convolution fusion | flops 319942272 | bytes 24291072 | tf_op jit(solution)/shard_map/while/body/eval_jaxpr/qhe,khe->hqk/dot_general | solution.py:70
  459.3 9.9 multiply_convert_fusion
  529.6 16.4 %copy.61 = bf16[1,6312,2,192]{3,2,0,1:T(2,128)(2,1)} copy(bf16[1,6312,2,192]{1,3,2,0:T(8,128)(2,1)} %pad_maximum_fusion) | data formatting | bytes 9695232 | tf_op jit(solution)/shard_map/stack | solution.py:275
  560.5 13.6 %reduce-scatter.36.cloned.1.call-done = f32[96,192]{1,0:T(8,128)} async-done(((f32[768,192]{1,0:T(8,128)}), f32[96,192]{1,0:T(8,128)}) %reduce-scatter.36.cloned.1.call-update) | async-done | bytes 73744
  575.7 63.7 %reduce-scatter.28.cloned.1.call-done = f32[96,192]{1,0:T(8,128)} async-done(((f32[768,192]{1,0:T(8,128)}), f32[96,192]{1,0:T(8,128)}) %reduce-scatter.28.cloned.1.call-update) | async-done | bytes 73744
  641.1 64.0 %reduce-scatter.32.cloned.1.call-done = f32[96,192]{1,0:T(8,128)} async-done(((f32[768,192]{1,0:T(8,128)}), f32[96,192]{1,0:T(8,128)}) %reduce-scatter.32.cloned.1.call-update) | async-done | bytes 73744
  706.7 65.4 %reduce-scatter.30.cloned.1.call-done = f32[96,384]{1,0:T(8,128)} async-done(((f32[768,384]{1,0:T(8,128)}), f32[96,384]{1,0:T(8,128)}) %reduce-scatter.30.cloned.1.call-update) | async-done | bytes 147472
  774.0 68.6 %reduce-scatter.34.cloned.1.call-done = f32[96,576]{1,0:T(8,128)} async-done(((f32[768,576]{1,0:T(8,128)}), f32[96,576]{1,0:T(8,128)}) %reduce-scatter.34.cloned.1.call-update) | async-done | bytes 221200
  844.6 17.2 %copy.62 = bf16[1,4,1578,2,192]{2,4,1,3,0:T(8,128)(2,1)} copy(bf16[1,4,1578,2,192]{4,3,2,1,0:T(2,128)(2,1)} %bitcast.46) | data formatting | bytes 9695232 | tf_op jit(solution)/shard_map/all_to_all | solution.py:280
  867.0 9.0 fusion.13
  885.4 37.7 %all-reduce.1 = (f32[2,2,192]{2,1,0:T(2,128)}, f32[2,768]{1,0:T(2,128)}, f32[2,2,192]{2,1,0:T(2,128)}, f32[5,192]{1,0:T(8,128)}, f32[5,192]{1,0:T(8,128)}) all-reduce(f32[2,2,192]{2,1,0:T(2,128)S(1)} %pad_maximum_fusion.2, f32[2,768]{1,0:T(2,128)S(1)} %pad_maximum_fusion.1, ...), channel_id=1, replica_groups=mesh['dp'=8,'head'=4] {'dp'}, use_global_device_ids=true, to_apply=%region_47.48 | all-reduce | flops 4992 | bytes 39936 | tf_op jit(solution)/shard_map/psum | solution.py:311
  928.4 12.5 %reduce-scatter.24.cloned.1.call-done = f32[96,768]{1,0:T(8,128)} async-done(((f32[768,768]{1,0:T(8,128)}), f32[96,768]{1,0:T(8,128)}) %reduce-scatter.24.cloned.1.call-update) | async-done | bytes 294928 | tf_op jit(solution)/shard_map/reduce_scatter | solution.py:322
  940.9 72.7 %reduce-scatter.26.cloned.1.call-done = f32[768,96]{0,1:T(8,128)} async-done(((f32[768,768]{0,1:T(8,128)}), f32[768,96]{0,1:T(8,128)}) %reduce-scatter.26.cloned.1.call-update) | async-done | bytes 294928 | tf_op jit(solution)/shard_map/reduce_scatter | solution.py:323
  1013.6 72.9 %reduce-scatter.20.cloned.1.call-done = f32[96,768]{1,0:T(8,128)} async-done(((f32[768,768]{1,0:T(8,128)}), f32[96,768]{1,0:T(8,128)}) %reduce-scatter.20.cloned.1.call-update) | async-done | bytes 294928 | tf_op jit(solution)/shard_map/reduce_scatter | solution.py:318
  1086.5 72.8 %reduce-scatter.22.cloned.1.call-done = f32[768,96]{0,1:T(8,128)} async-done(((f32[768,768]{0,1:T(8,128)}), f32[768,96]{0,1:T(8,128)}) %reduce-scatter.22.cloned.1.call-update) | async-done | bytes 294928 | tf_op jit(solution)/shard_map/reduce_scatter | solution.py:319
  (381 shorter events, 198.4 us)
Async XLA Ops:
  7.2 229.9 %copy-start = (bf16[768,768]{1,0:T(8,128)(2,1)S(1)}, bf16[768,768]{1,0:T(8,128)(2,1)}, u32[]{:S(2)}) copy-start(bf16[768,768]{1,0:T(8,128)(2,1)} %param.27) | copy-start | bytes 3538948
  7.3 144.2 %all-gather.3.cloned.1.call-start = ((), (), s32[]{:S(2)}) async-start(), calls=%async_computation.10 | async-start | bytes 24238080 | tf_op jit(solution)/shard_map/all_gather | solution.py:149
  25.7 207.0 %all-reduce.12.cloned.1.call-start = ((), (), s32[]{:S(2)}) async-start(), calls=%async_computation.11 | async-start | bytes 393216 | tf_op jit(solution)/shard_map/psum | solution.py:39
  25.9 168.6 %copy-start.92 = (f32[3,64]{1,0:T(4,128)}, f32[3,64]{1,0:T(4,128)S(1)}, u32[]{:S(2)}) copy-start(f32[3,64]{1,0:T(4,128)S(1)} %add.344) | copy-start | bytes 2308
  27.9 207.1 %copy-start.47 = (f32[768]{0:T(1024)}, f32[768]{0:T(1024)S(1)}, u32[]{:S(2)}) copy-start(f32[768]{0:T(1024)S(1)} %get-tuple-element.151) | copy-start | bytes 9220
  28.7 154.8 %copy-start.35 = (bf16[128,192]{0,1:T(8,128)(2,1)}, bf16[128,192]{0,1:T(8,128)(2,1)S(1)}, u32[]{:S(2)}) copy-start(bf16[128,192]{0,1:T(8,128)(2,1)S(1)} %fusion.33) | copy-start | bytes 147460
  200.6 69.8 %all-reduce.14.cloned.1.call-start = ((), (), s32[]{:S(2)}) async-start(), calls=%async_computation.12 | async-start | bytes 393216 | tf_op jit(solution)/shard_map/psum | solution.py:39
  238.2 74.1 %all-reduce.16.cloned.1.call-start = ((), (), s32[]{:S(2)}) async-start(), calls=%async_computation.13 | async-start | bytes 393216 | tf_op jit(solution)/shard_map/psum | solution.py:39
  280.1 72.6 %all-reduce.18.cloned.1.call-start = ((), (), s32[]{:S(2)}) async-start(), calls=%async_computation.14 | async-start | bytes 393216 | tf_op jit(solution)/shard_map/psum | solution.py:43
  320.6 80.8 %all-reduce.20.cloned.1.call-start = ((), (), s32[]{:S(2)}) async-start(), calls=%async_computation.15 | async-start | bytes 393216 | tf_op jit(solution)/shard_map/psum | solution.py:43
  369.1 72.9 %all-reduce.22.cloned.1.call-start = ((), (), s32[]{:S(2)}) async-start(), calls=%async_computation.16 | async-start | bytes 393216 | tf_op jit(solution)/shard_map/psum | solution.py:43
  409.9 146.2 %all-reduce.24.cloned.1.call-start = ((), (), s32[]{:S(2)}) async-start(), calls=%async_computation.27 | async-start | bytes 786432 | tf_op jit(solution)/shard_map/psum | solution.py:39
  474.5 99.6 %reduce-scatter.36.cloned.1.call-start = ((), (), s32[]{:S(2)}) async-start(), calls=%async_computation.26 | async-start | bytes 884736
  475.8 163.7 %reduce-scatter.28.cloned.1.call-start = ((), (), s32[]{:S(2)}) async-start(), calls=%async_computation.22 | async-start | bytes 884736
  478.4 226.7 %reduce-scatter.32.cloned.1.call-start = ((), (), s32[]{:S(2)}) async-start(), calls=%async_computation.24 | async-start | bytes 884736
  485.4 286.7 %reduce-scatter.30.cloned.1.call-start = ((), (), s32[]{:S(2)}) async-start(), calls=%async_computation.23 | async-start | bytes 1327104
  506.9 335.6 %reduce-scatter.34.cloned.1.call-start = ((), (), s32[]{:S(2)}) async-start(), calls=%async_computation.25 | async-start | bytes 2211840
  517.7 349.4 %all-gather.5.cloned.1.call-start = ((), (), s32[]{:S(2)}) async-start(), calls=%async_computation.17 | async-start | bytes 2949120 | tf_op jit(solution)/shard_map/all_gather | solution.py:150
  518.3 422.6 %reduce-scatter.24.cloned.1.call-start = ((), (), s32[]{:S(2)}) async-start(), calls=%async_computation.20 | async-start | bytes 2654208 | tf_op jit(solution)/shard_map/reduce_scatter | solution.py:322
  520.4 493.2 %reduce-scatter.26.cloned.1.call-start = ((), (), s32[]{:S(2)}) async-start(), calls=%async_computation.21 | async-start | bytes 2654208 | tf_op jit(solution)/shard_map/reduce_scatter | solution.py:323
  522.4 564.1 %reduce-scatter.20.cloned.1.call-start = ((), (), s32[]{:S(2)}) async-start(), calls=%async_computation.18 | async-start | bytes 2654208 | tf_op jit(solution)/shard_map/reduce_scatter | solution.py:318
  546.1 298.5 %all-to-all-start = ((bf16[1,6312,2,192]{3,2,0,1:T(2,128)(2,1)}), bf16[1,6312,2,192]{3,2,0,1:T(2,128)(2,1)}, u32[]{:S(2)}, u32[]{:S(2)}) async-start(bf16[1,6312,2,192]{3,2,0,1:T(2,128)(2,1)} %copy.61), calls=%async_computation | async-start | bytes 12926976 | tf_op jit(solution)/shard_map/all_to_all | solution.py:280
  551.5 607.7 %reduce-scatter.22.cloned.1.call-start = ((), (), s32[]{:S(2)}) async-start(), calls=%async_computation.19 | async-start | bytes 2654208 | tf_op jit(solution)/shard_map/reduce_scatter | solution.py:319
  923.1 236.1 %copy-start.1 = (bf16[768,768]{1,0:T(8,128)(2,1)S(1)}, bf16[768,768]{1,0:T(8,128)(2,1)}, u32[]{:S(2)}) copy-start(bf16[768,768]{1,0:T(8,128)(2,1)} %param.27) | copy-start | bytes 3538948
  (96 other events, 2352.8 us)
Sparse Core Ops, SparseCore 0:
  25.9 125.5 all-gather.2
  200.7 31.9 all-reduce.11
  238.3 32.0 all-reduce.13
  280.2 32.0 all-reduce.15
  320.7 32.0 all-reduce.17
  369.2 32.0 all-reduce.19
  410.0 32.0 all-reduce.21
  474.6 32.8 all-reduce.23
  510.8 63.2 reduce-scatter.35
  577.3 62.1 reduce-scatter.27
  642.8 62.2 reduce-scatter.31
  708.3 63.7 reduce-scatter.29
  776.1 66.3 reduce-scatter.33
  844.0 22.9 all-gather.4
  870.9 69.9 reduce-scatter.23
  944.8 68.7 reduce-scatter.25
  1017.5 68.9 reduce-scatter.19
  1090.4 68.7 reduce-scatter.21
where the time goes:
time: 1170 us
  waiting for transfers between devices  823 us (70%)
  matrix products  102 us (9%)
  local copies, waits for them, and re-layouts  92.2 us (8%)
  other arithmetic  81.6 us (7%)
  blocking collectives  44.1 us (4%)
  between operations  16.7 us (1%)
    unnamed x23, waiting for transfers between devices  276 us
    all_gather x1, waiting for transfers between devices, local(): lax.all_gather(tokens, 'head', axis=1, tiled=True)  123 us
    psum x4, waiting for transfers between devices, join_heads(): lax.psum(partial_sum.astype(jnp.bfloat16), 'head').astype(jnp.float32)  94.2 us
    psum x3, waiting for transfers between devices, join_back(): lax.psum(partial_sum.astype(jnp.bfloat16), 'head').astype(jnp.float32)  93.6 us
    reduce_scatter x1, waiting for transfers between devices, local(): lax.psum_scatter(grad_cross_up, 'dp', scatter_dimension=0, tiled=True)  72.9 us
    reduce_scatter x1, waiting for transfers between devices, local(): lax.psum_scatter(grad_cross_down, 'dp', scatter_dimension=1, tiled=True)  72.8 us
    reduce_scatter x1, waiting for transfers between devices, local(): lax.psum_scatter(grad_self_down, 'dp', scatter_dimension=1, tiled=True)  72.7 us
    unnamed x214, local copies, waits for them, and re-layouts  51.9 us
  transfers between devices with their start and end apart: 19, of which 17 were waited for; matrix products, arithmetic and copies ran while one was open for 11% of the time, Pallas kernels for 0%

commit v1 on v0

--- a/solution.py
+++ b/solution.py
@@ -311,32 +311,40 @@
     small_sums = lax.psum(
         (grad_head_bias, grad_up_bias, grad_out_bias, grad_norm_gain, grad_norm_bias), "dp"
     )
-    combined = (
-        lax.psum_scatter(grad_cross_q, "dp", scatter_dimension=1, tiled=True),
-        lax.psum_scatter(grad_cross_kv, "dp", scatter_dimension=2, tiled=True),
-        lax.psum_scatter(grad_cross_out, "dp", scatter_dimension=1, tiled=True),
-        lax.psum_scatter(grad_cross_up, "dp", scatter_dimension=0, tiled=True),
-        lax.psum_scatter(grad_cross_down, "dp", scatter_dimension=1, tiled=True),
-        lax.psum_scatter(grad_self_qkv, "dp", scatter_dimension=2, tiled=True),
-        lax.psum_scatter(grad_self_out, "dp", scatter_dimension=1, tiled=True),
-        lax.psum_scatter(grad_self_up, "dp", scatter_dimension=0, tiled=True),
-        lax.psum_scatter(grad_self_down, "dp", scatter_dimension=1, tiled=True),
-    )
-    cross_sums = combined[:5]
-    self_sums = combined[5:]
+    pieces = [
+        grad_cross_q.T,
+        grad_cross_kv[0].T,
+        grad_cross_kv[1].T,
+        grad_cross_out.T,
+        grad_self_qkv[0].T,
+        grad_self_qkv[1].T,
+        grad_self_qkv[2].T,
+        grad_self_out.T,
+        grad_cross_up,
+        grad_cross_down.T,
+        grad_self_up,
+        grad_self_down.T,
+    ]
+    packed = jnp.concatenate([piece.astype(jnp.bfloat16) for piece in pieces], axis=1)
+    summed = lax.psum_scatter(packed, "dp", scatter_dimension=0, tiled=True).astype(jnp.float32)
+    sums = []
+    start = 0
+    for piece in pieces:
+        sums.append(summed[:, start : start + piece.shape[1]])
+        start += piece.shape[1]
     return (
         latents_out,
         grad_tokens,
         grad_latents,
-        cross_sums[0],
-        cross_sums[1],
-        cross_sums[2],
-        cross_sums[3],
-        cross_sums[4],
-        self_sums[0],
-        self_sums[1],
-        self_sums[2],
-        self_sums[3],
+        sums[0].T,
+        jnp.stack([sums[1].T, sums[2].T]),
+        sums[3].T,
+        sums[8],
+        sums[9].T,
+        jnp.stack([sums[4].T, sums[5].T, sums[6].T]),
+        sums[7].T,
+        sums[10],
+        sums[11].T,
         small_sums[0],
         small_sums[1],
         small_sums[2],

time: 1170 us -> 720 us (0.62)
  waiting for transfers between devices: 823 us -> 377 us
    unnamed x23 -> x11, waiting for transfers between devices: 276 us -> 0.83 us
    reduce_scatter x4 -> x0, waiting for transfers between devices: 231 us -> none  [the longest x1 72.9 us: local(): lax.psum_scatter(grad_cross_up, 'dp', scatter_dimension=0, tiled=True)]
    all_to_all x1, waiting for transfers between devices: 0.01 us -> 65.7 us  [local(): lax.all_to_all(grad_pair, 'head', split_axis=1, concat_axis=3, tiled=True)]
    unnamed x214 -> x232, local copies, waits for them, and re-layouts: 51.9 us -> 45.2 us
  transfers between devices with their start and end apart: 19 -> 11, of which waited for: 17 -> 8; matrix products, arithmetic and copies ran while one was open for 11% -> 15% of each run, Pallas kernels for 0% -> 0%
where the time goes in v1:
time: 720 us; the launch traced here: 713 us
  waiting for transfers between devices  377 us (52%)
  matrix products  95.7 us (13%)
  local copies, waits for them, and re-layouts  86.2 us (12%)
  other arithmetic  85.4 us (12%)
  blocking collectives  44.5 us (6%)
  between operations  16.9 us (2%)
    all_gather x1, waiting for transfers between devices, local(): lax.all_gather(tokens, 'head', axis=1, tiled=True)  123 us
    psum x4, waiting for transfers between devices, join_heads(): lax.psum(partial_sum.astype(jnp.bfloat16), 'head').astype(jnp.float32)  94.3 us
    psum x3, waiting for transfers between devices, join_back(): lax.psum(partial_sum.astype(jnp.bfloat16), 'head').astype(jnp.float32)  94 us
    all_to_all x1, waiting for transfers between devices, local(): lax.all_to_all(grad_pair, 'head', split_axis=1, concat_axis=3, tiled=True)  65.7 us
    unnamed x232, local copies, waits for them, and re-layouts  45.2 us
    psum x1, blocking collectives, local(): lax.psum((grad_head_bias, grad_up_bias, grad_out_bias, grad_norm_gain, gr...  38.4 us
    all_to_all x1, local copies, waits for them, and re-layouts, local(): lax.all_to_all(grad_pair, 'head', split_axis=1, concat_axis=3, tiled=True)  17 us
    another operation x1, local copies, waits for them, and re-layouts, local(): jnp.stack([merge_heads(cross_grads[1]), merge_heads(cross_grads[2])], axi...  16.4 us
  transfers between devices with their start and end apart: 11, of which 8 were waited for; matrix products, arithmetic and copies ran while one was open for 15% of the time, Pallas kernels for 0%

profile of v1, /device:TPU:0, one launch (start us, length us, event | category | flops | bytes accessed | tf_op | source)
XLA Modules:
  0.0 712.6 jit_solution(15768888642467319990)
XLA Ops:
  7.3 18.4 %copy.67 = bf16[1,1578,768]{2,0,1:T(2,128)(2,1)} copy(bf16[1,1578,768]{2,1,0:T(8,128)(2,1)} %param.19) | data formatting | bytes 4847616 | tf_op args[0]
  28.8 122.7 %all-gather.3.cloned.1.call-done = bf16[1,6312,768]{2,0,1:T(2,128)(2,1)} async-done(((bf16[1,1578,768]{2,0,1:T(2,128)(2,1)}), bf16[1,6312,768]{2,0,1:T(2,128)(2,1)}) %all-gather.3.cloned.1.call-update) | async-done | bytes 9695248 | tf_op jit(solution)/shard_map/all_gather | solution.py:149
  151.5 7.5 %convert_reduce_fusion = f32[6312]{0:T(1024)S(1)} fusion(bf16[1,6312,768]{2,0,1:T(2,128)(2,1)} %all-gather.3.cloned.1.call-done), kind=kLoop, calls=%fused_computation.3 | loop fusion | flops 9688920 | bytes 9720480 | tf_op jit(solution)/shard_map/reduce_sum | solution.py:153
  159.0 14.1 %fusion.4 = f32[6312]{0:T(1024)S(1)} fusion(f32[6312]{0:T(1024)S(1)} %broadcast_multiply_fusion, bf16[1,6312,768]{2,0,1:T(2,128)(2,1)} %all-gather.3.cloned.1.call-done), kind=kLoop, calls=%fused_computation.6 | loop fusion | flops 19384152 | bytes 9745728 | tf_op jit(solution)/shard_map/reduce_sum | solution.py:155
  173.2 5.9 fusion.10
  188.6 6.2 fusion.167
  201.7 31.3 %all-reduce.12.cloned.1.call-done = bf16[1,128,768]{2,1,0:T(8,128)(2,1)} async-done(((bf16[1,128,768]{2,1,0:T(8,128)(2,1)}), bf16[1,128,768]{2,1,0:T(8,128)(2,1)}) %all-reduce.12.cloned.1.call-update) | async-done | bytes 196624 | tf_op jit(solution)/shard_map/psum | solution.py:39
  239.9 30.8 %all-reduce.14.cloned.1.call-done = bf16[1,128,768]{2,1,0:T(8,128)(2,1)} async-done(((bf16[1,128,768]{2,1,0:T(8,128)(2,1)}), bf16[1,128,768]{2,1,0:T(8,128)(2,1)}) %all-reduce.14.cloned.1.call-update) | async-done | bytes 196624 | tf_op jit(solution)/shard_map/psum | solution.py:39
  280.5 32.1 %all-reduce.16.cloned.1.call-done = bf16[1,128,768]{2,1,0:T(8,128)(2,1)} async-done(((bf16[1,128,768]{2,1,0:T(8,128)(2,1)}), bf16[1,128,768]{2,1,0:T(8,128)(2,1)}) %all-reduce.16.cloned.1.call-update) | async-done | bytes 196624 | tf_op jit(solution)/shard_map/psum | solution.py:39
  321.0 32.1 %all-reduce.18.cloned.1.call-done = bf16[1,128,768]{2,1,0:T(8,128)(2,1)} async-done(((bf16[1,128,768]{2,1,0:T(8,128)(2,1)}), bf16[1,128,768]{2,1,0:T(8,128)(2,1)}) %all-reduce.18.cloned.1.call-update) | async-done | bytes 196624 | tf_op jit(solution)/shard_map/psum | solution.py:43
  369.4 32.1 %all-reduce.20.cloned.1.call-done = bf16[1,128,768]{2,1,0:T(8,128)(2,1)} async-done(((bf16[1,128,768]{2,1,0:T(8,128)(2,1)}), bf16[1,128,768]{2,1,0:T(8,128)(2,1)}) %all-reduce.20.cloned.1.call-update) | async-done | bytes 196624 | tf_op jit(solution)/shard_map/psum | solution.py:43
  412.6 29.7 %all-reduce.22.cloned.1.call-done = bf16[1,128,768]{2,1,0:T(8,128)(2,1)} async-done(((bf16[1,128,768]{2,1,0:T(8,128)(2,1)}), bf16[1,128,768]{2,1,0:T(8,128)(2,1)}) %all-reduce.22.cloned.1.call-update) | async-done | bytes 196624 | tf_op jit(solution)/shard_map/psum | solution.py:43
  449.5 11.8 %multiply_reduce_fusion = (f32[3,128]{1,0:T(4,128)S(1)}, f32[3,128,6312]{1,2,0:T(8,128)}) fusion(f32[3,128,6312]{1,2,0:T(8,128)} %get-tuple-element.268, f32[3,128]{1,0:T(4,128)S(1)} %copy-done.87, bf16[128,3,64]{0,2,1:T(8,128)(2,1)S(1)} %bitcast.305, f32[6312,3,64]{0,2,1:T(8,128)} %bitcast.281, f32[3,64]{1,0:T(4,128)S(1)} %copy-done.98), kind=kOutput, calls=%fused_computation.16 | convolution fusion | flops 319942272 | bytes 24291072 | tf_op jit(solution)/shard_map/while/body/eval_jaxpr/qhe,khe->hqk/dot_general | solution.py:70
  461.3 9.9 %multiply_convert_fusion = bf16[3,128,6312]{1,2,0:T(8,128)(2,1)} fusion(f32[3,128,6312]{1,2,0:T(8,128)} %get-tuple-element.274, f32[3,128]{1,0:T(4,128)S(1)} %get-tuple-element.273, f32[3,128,6312]{1,2,0:T(8,128)} %get-tuple-element.268, f32[3,128]{1,0:T(4,128)S(1)} %copy-done.87), kind=kLoop, calls=%fused_computation.15 | loop fusion | flops 9695232 | bytes 24241152 | tf_op jit(solution)/shard_map/while/body/eval_jaxpr/convert_element_type | solution.py:72
  478.7 6.3 convert_reduce_fusion.1
  488.0 7.9 %fusion.26 = bf16[2,192,768]{2,1,0:T(8,128)(2,1)S(1)} fusion(bf16[6312,768,1]{1,0,2:T(8,128)(2,1)} %copy-done.8, bf16[1,6312,1,192]{1,3,2,0:T(8,128)(2,1)S(1)} %bitcast.282, bf16[1,6312,1,192]{1,3,2,0:T(8,128)(2,1)S(1)} %bitcast.277), kind=kOutput, calls=%fused_computation.50 | convolution fusion | flops 3725687808 | bytes 15132672 | tf_op jit(solution)/shard_map/cld,clkw->kwd/dot_general | solution.py:276
  507.9 10.3 %copy.85 = bf16[768,4608]{1,0:T(8,128)(2,1)} copy(bf16[768,4608]{0,1:T(8,128)(2,1)} %fusion.25) | data formatting | bytes 14155776
  518.3 5.6 pad_maximum_fusion
  523.9 16.4 %copy.73 = bf16[1,6312,2,192]{3,2,0,1:T(2,128)(2,1)} copy(bf16[1,6312,2,192]{1,3,2,0:T(8,128)(2,1)} %pad_maximum_fusion) | data formatting | bytes 9695232 | tf_op jit(solution)/shard_map/stack | solution.py:275
  552.9 65.7 %all-to-all-done = bf16[1,6312,2,192]{3,2,0,1:T(2,128)(2,1)} async-done(((bf16[1,6312,2,192]{3,2,0,1:T(2,128)(2,1)}), bf16[1,6312,2,192]{3,2,0,1:T(2,128)(2,1)}, u32[]{:S(2)}, u32[]{:S(2)}) %all-to-all-start) | async-done | bytes 4847648 | tf_op jit(solution)/shard_map/all_to_all | solution.py:280
  618.6 17.0 %copy.74 = bf16[1,4,1578,2,192]{2,4,1,3,0:T(8,128)(2,1)} copy(bf16[1,4,1578,2,192]{4,3,2,1,0:T(2,128)(2,1)} %bitcast.46) | data formatting | bytes 9695232 | tf_op jit(solution)/shard_map/all_to_all | solution.py:280
  635.6 9.5 %fusion.13 = (f32[768]{0:T(1024)S(1)}, f32[1578]{0:T(1024)S(1)}, f32[1578,768,1]{1,0,2:T(8,128)S(1)}) fusion(bf16[1,1578,768]{2,1,0:T(8,128)(2,1)} %param.19, f32[1578]{0:T(1024)S(1)} %dynamic_slice.65, f32[1578]{0:T(1024)S(1)} %dynamic_slice.64, f32[768]{0:T(1024)S(1)} %copy-done.44, bf16[1578,2,768]{0,2,1:T(8,128)(2,1)} %bitcast.279, ...), kind=kOutput, calls=%fused_computation.26 | convolution fusion | flops 3732662016 | bytes 14503416 | tf_op jit(solution)/shard_map/clkw,kwd->cld/dot_general | solution.py:281
  648.0 6.2 all-reduce.2
  654.4 38.4 %all-reduce.1 = (f32[2,2,192]{2,1,0:T(2,128)}, f32[2,768]{1,0:T(2,128)}, f32[2,2,192]{2,1,0:T(2,128)}, f32[5,192]{1,0:T(8,128)}, f32[5,192]{1,0:T(8,128)}) all-reduce(f32[2,2,192]{2,1,0:T(2,128)S(1)} %pad_maximum_fusion.4, f32[2,768]{1,0:T(2,128)S(1)} %pad_maximum_fusion.3, ...), channel_id=1, replica_groups=mesh['dp'=8,'head'=4] {'dp'}, use_global_device_ids=true, to_apply=%region_39.40 | all-reduce | flops 4992 | bytes 39936 | tf_op jit(solution)/shard_map/psum | solution.py:311
  (382 shorter events, 127.7 us)
Async XLA Ops:
  7.2 230.3 %copy-start = (bf16[768,768]{1,0:T(8,128)(2,1)S(1)}, bf16[768,768]{1,0:T(8,128)(2,1)}, u32[]{:S(2)}) copy-start(bf16[768,768]{1,0:T(8,128)(2,1)} %param.27) | copy-start | bytes 3538948
  7.3 144.2 %all-gather.3.cloned.1.call-start = ((), (), s32[]{:S(2)}) async-start(), calls=%async_computation.2 | async-start | bytes 24238080 | tf_op jit(solution)/shard_map/all_gather | solution.py:149
  25.7 207.3 %all-reduce.12.cloned.1.call-start = ((), (), s32[]{:S(2)}) async-start(), calls=%async_computation.3 | async-start | bytes 393216 | tf_op jit(solution)/shard_map/psum | solution.py:39
  25.9 168.9 %copy-start.97 = (f32[3,64]{1,0:T(4,128)}, f32[3,64]{1,0:T(4,128)S(1)}, u32[]{:S(2)}) copy-start(f32[3,64]{1,0:T(4,128)S(1)} %add.328) | copy-start | bytes 2308
  27.9 131.0 %copy-start.89 = (f32[768]{0:T(1024)}, f32[768]{0:T(1024)S(1)}, u32[]{:S(2)}) copy-start(f32[768]{0:T(1024)S(1)} %get-tuple-element.220) | copy-start | bytes 9220
  27.9 207.4 %copy-start.48 = (f32[768]{0:T(1024)}, f32[768]{0:T(1024)S(1)}, u32[]{:S(2)}) copy-start(f32[768]{0:T(1024)S(1)} %get-tuple-element.219) | copy-start | bytes 9220
  28.0 130.9 %copy-start.45 = (f32[768]{0:T(1024)}, f32[768]{0:T(1024)S(1)}, u32[]{:S(2)}) copy-start(f32[768]{0:T(1024)S(1)} %get-tuple-element.215) | copy-start | bytes 9220
  28.0 145.1 %copy-start.43 = (f32[768]{0:T(1024)}, f32[768]{0:T(1024)S(1)}, u32[]{:S(2)}) copy-start(f32[768]{0:T(1024)S(1)} %get-tuple-element.216) | copy-start | bytes 9220
  28.1 130.8 %copy-start.77 = (f32[128]{0:T(128)}, f32[128]{0:T(128)S(1)}, u32[]{:S(2)}) copy-start(f32[128]{0:T(128)S(1)} %broadcast_multiply_fusion.6) | copy-start | bytes 1540
  28.4 130.6 %copy-start.101 = (f32[128]{0:T(128)}, f32[128]{0:T(128)S(1)}, u32[]{:S(2)}) copy-start(f32[128]{0:T(128)S(1)} %fusion.86) | copy-start | bytes 1540
  28.4 130.6 %copy-start.94 = (f32[128]{0:T(128)}, f32[128]{0:T(128)S(1)}, u32[]{:S(2)}) copy-start(f32[128]{0:T(128)S(1)} %fusion.133) | copy-start | bytes 1540
  28.7 155.1 %copy-start.35 = (bf16[128,192]{0,1:T(8,128)(2,1)}, bf16[128,192]{0,1:T(8,128)(2,1)S(1)}, u32[]{:S(2)}) copy-start(bf16[128,192]{0,1:T(8,128)(2,1)S(1)} %fusion.44) | copy-start | bytes 147460
  200.9 69.8 %all-reduce.14.cloned.1.call-start = ((), (), s32[]{:S(2)}) async-start(), calls=%async_computation.4 | async-start | bytes 393216 | tf_op jit(solution)/shard_map/psum | solution.py:39
  238.5 74.1 %all-reduce.16.cloned.1.call-start = ((), (), s32[]{:S(2)}) async-start(), calls=%async_computation.5 | async-start | bytes 393216 | tf_op jit(solution)/shard_map/psum | solution.py:39
  280.4 72.6 %all-reduce.18.cloned.1.call-start = ((), (), s32[]{:S(2)}) async-start(), calls=%async_computation.6 | async-start | bytes 393216 | tf_op jit(solution)/shard_map/psum | solution.py:43
  320.9 82.6 %copy-start.53 = (f32[128]{0:T(128)S(1)}, f32[128]{0:T(128)}, u32[]{:S(2)}) copy-start(f32[128]{0:T(128)} %copy-done.52) | copy-start | bytes 1540
  320.9 82.6 %copy-start.75 = (f32[128]{0:T(128)S(1)}, f32[128]{0:T(128)}, u32[]{:S(2)}) copy-start(f32[128]{0:T(128)} %copy-done.74) | copy-start | bytes 1540
  320.9 86.1 %copy-start.15 = (f32[128,768]{1,0:T(8,128)S(1)}, f32[128,768]{1,0:T(8,128)}, u32[]{:S(2)}) copy-start(f32[128,768]{1,0:T(8,128)} %copy-done.14) | copy-start | bytes 1179652
  320.9 80.7 %all-reduce.20.cloned.1.call-start = ((), (), s32[]{:S(2)}) async-start(), calls=%async_computation.7 | async-start | bytes 393216 | tf_op jit(solution)/shard_map/psum | solution.py:43
  369.4 72.9 %all-reduce.22.cloned.1.call-start = ((), (), s32[]{:S(2)}) async-start(), calls=%async_computation.8 | async-start | bytes 393216 | tf_op jit(solution)/shard_map/psum | solution.py:43
  410.1 138.3 %all-reduce.24.cloned.1.call-start = ((), (), s32[]{:S(2)}) async-start(), calls=%async_computation.11 | async-start | bytes 786432 | tf_op jit(solution)/shard_map/psum | solution.py:39
  477.1 158.5 %all-gather.5.cloned.1.call-start = ((), (), s32[]{:S(2)}) async-start(), calls=%async_computation.9 | async-start | bytes 2949120 | tf_op jit(solution)/shard_map/all_gather | solution.py:150
  477.8 219.9 %reduce-scatter.4.cloned.1.call-start = ((), (), s32[]{:S(2)}) async-start(), calls=%async_computation.10 | async-start | bytes 7962624
  540.5 78.1 %all-to-all-start = ((bf16[1,6312,2,192]{3,2,0,1:T(2,128)(2,1)}), bf16[1,6312,2,192]{3,2,0,1:T(2,128)(2,1)}, u32[]{:S(2)}, u32[]{:S(2)}) async-start(bf16[1,6312,2,192]{3,2,0,1:T(2,128)(2,1)} %copy.73), calls=%async_computation | async-start | bytes 12926976 | tf_op jit(solution)/shard_map/all_to_all | solution.py:280
  (97 other events, 1553.9 us)
Sparse Core Ops, SparseCore 0:
  25.9 125.5 all-gather.2
  201.0 32.0 all-reduce.11
  238.6 32.0 all-reduce.13
  280.6 32.0 all-reduce.15
  321.0 32.0 all-reduce.17
  369.5 32.0 all-reduce.19
  410.2 32.0 all-reduce.21
  477.2 32.9 all-reduce.23
  511.7 24.0 all-gather.4
  539.3 129.7 reduce-scatter.3
